TPU v7x, 512 devices: a whole 4x8x8 slice. The times are simulated.
512 devices in a mesh: dp: 64 (over y, x, core), mp: 8 (over z).
Axes of the slice: x: 4, y: 8, z: 8, core: 2. Of those that a mesh axis runs over, the one named last changes fastest.
Arguments:
- hidden: bfloat16 [960, 128, 2048], P('dp', None, 'mp'), may hold values from -6 to 6
- attn_out: bfloat16 [960, 128, 2048], P('dp', None, 'mp'), may hold values from -6 to 6
- out_proj: bfloat16 [2048, 2048], P(None, 'mp'), may hold values from -0.125 to 0.125
- norm_gain: float32 [2048], P('mp'), may hold values from 0.1 to 1.9
- reward_proj: float32 [2048, 8], P('mp'), may hold values from -0.125 to 0.125
- block_seq: int32 [960], replicated, may hold values from -1 to 383, as said below
- block_dest: int32 [960], replicated, may hold values from -1 to 639, as said below
- lengths: int32 [384], replicated, may hold values from 1 to 512, as said below
Outputs:
- token_rewards: float32 [640, 8, 128], P('dp')
- advantages: float32 [384], P('dp')
Inputs may be any that keep to these rules, and one draw needn't show every extreme that they name: `block_seq`: used slots of each index of dp come first in its 15 slots, the rest hold -1; each index of dp holds 1 to 15 used slots and some index holds exactly 15. Read over used slots in slot order, response numbers never fall, every response appears, and each has 1 to 4 blocks. `block_dest`: exactly the used slots (those of block_seq that are not -1) hold a destination; every owned slot of every owner is named exactly once, so each owner receives exactly 10 blocks; at most 1 block go from one index of dp to one owner, and that many in some pair. `lengths`: A response of n blocks has more than 128 * (n - 1) and at most 128 * n tokens.
All inputs are finite; a program needn't handle non-finite values.
Results may differ from a plain program's by a relative error of at most 0.0029.
Values may be sent and summed in bfloat16 or wider, within the bound.
No kernel may reach another device: no remote copies, remote signals or barrier semaphores. Data moves between devices by JAX's collectives and lax.ppermute only.
A program may use at most 64 MiB of HBM per device.

v0:
```python
import jax
import jax.numpy as jnp
from jax import lax
from jax.sharding import PartitionSpec as P

OWN_CAP = 10
norm_epsilon = 1e-05
stat_epsilon = 1e-06


def sent_to_all(value, axis):
    copies = jnp.broadcast_to(value, (lax.axis_size(axis), *value.shape))
    return lax.all_to_all(copies, axis, split_axis=0, concat_axis=0, tiled=True)


def of_everyone(value, axis):
    everything = sent_to_all(value, axis)
    return jnp.sum(everything, axis=0)


def packed_total(arrays, axis):
    ends = [0]
    for a in arrays:
        ends.append(ends[-1] + a.size)
    so_far = of_everyone(jnp.concatenate([a.ravel() for a in arrays]), axis)
    return tuple((so_far[b:e].reshape(a.shape) for a, b, e in zip(arrays, ends, ends[1:])))


def split_up(value, dim, peers):
    before, after = (value.shape[:dim], value.shape[dim + 1 :])
    return jnp.moveaxis(value.reshape(*before, peers, -1, *after), dim, 0)


def sent_and_summed(value, axis, dim):
    parts = split_up(value, dim, lax.axis_size(axis))
    arrived = lax.all_to_all(parts, axis, split_axis=0, concat_axis=0, tiled=True)
    return arrived.sum(axis=0)


def local(hidden, attn_out, out_proj, norm_gain, reward_proj, block_seq, block_dest, lengths):
    device_count = lax.axis_size("dp")
    device_rank = lax.axis_index("dp")
    slots_in = hidden.shape[0]
    block_len = hidden.shape[1]
    model_width = out_proj.shape[0]
    seq_count = lengths.shape[0]
    seq_local = seq_count // device_count
    slot_depth = (slots_in + device_count - 1) // device_count
    all_slots = jnp.arange(block_dest.shape[0], dtype=jnp.int32)
    local_dest = lax.dynamic_slice_in_dim(block_dest, device_rank * slots_in, slots_in)
    is_used = local_dest >= 0
    owner_rank = jnp.where(is_used, local_dest // OWN_CAP, -1)
    local_slots = jnp.arange(slots_in, dtype=jnp.int32)
    earlier = (
        (owner_rank[None, :] == owner_rank[:, None])
        & (local_slots[None, :] < local_slots[:, None])
        & is_used[None, :]
    )
    send_row = jnp.where(is_used, owner_rank * slot_depth + earlier.sum(axis=1), -1)
    buffer_rows = jnp.arange(device_count * slot_depth, dtype=jnp.int32)
    selector = (send_row[None, :] == buffer_rows[:, None]).astype(jnp.bfloat16)
    targets = device_rank * OWN_CAP + jnp.arange(OWN_CAP, dtype=jnp.int32)
    matches = block_dest[None, :] == targets[:, None]
    source_slot = jnp.sum(jnp.where(matches, all_slots[None, :], 0), axis=1)
    source_rank = source_slot // slots_in
    before = (block_dest[None, :] >= 0) & (block_dest[None, :] // OWN_CAP == device_rank)
    before = (
        before
        & (all_slots[None, :] >= (source_rank * slots_in)[:, None])
        & (all_slots[None, :] < source_slot[:, None])
    )
    recv_row = source_rank * slot_depth + before.sum(axis=1)
    seq_own = jnp.sum(jnp.where(matches, block_seq[None, :], 0), axis=1)
    earlier_same = (block_seq[None, :] == seq_own[:, None]) & (
        all_slots[None, :] < source_slot[:, None]
    )
    seq_rank = earlier_same.sum(axis=1)
    seq_ids = jnp.arange(seq_count, dtype=jnp.int32)
    member = seq_ids[:, None] == seq_own[None, :]
    own_length = jnp.sum(jnp.where(member, lengths[:, None], 0), axis=0)
    valid_tokens = jnp.minimum(block_len, own_length - block_len * seq_rank)
    projected = jnp.einsum(
        "btf,fc->btc",
        lax.all_gather(attn_out, "mp", axis=2, tiled=True),
        out_proj,
        preferred_element_type=jnp.float32,
    )
    local_resid = (hidden.astype(jnp.float32) + projected).astype(jnp.bfloat16)
    moved_resid = lax.all_to_all(
        jnp.einsum("rj,jtf->rtf", selector, local_resid, preferred_element_type=jnp.float32).astype(
            jnp.bfloat16
        ),
        "dp",
        split_axis=0,
        concat_axis=0,
        tiled=True,
    )
    residual = jnp.take(moved_resid, recv_row, axis=0)
    values = residual.astype(jnp.float32)
    squares = jnp.sum(values * values, axis=2)
    weighted = norm_gain[:, None] * reward_proj
    partial_value = jnp.einsum("btf,fh->bht", values, weighted, precision=lax.Precision.HIGHEST)
    squares, partial_value = packed_total((squares, partial_value), "mp")
    inverse_rms = lax.rsqrt(squares / model_width + norm_epsilon)
    live_tokens = (jnp.arange(block_len, dtype=jnp.int32)[None, :] < valid_tokens[:, None]).astype(
        jnp.float32
    )
    token_rewards = partial_value * (inverse_rms * live_tokens)[:, None, :]
    block_sums = jnp.sum(token_rewards, axis=2)
    seq_part = jnp.dot(member.astype(jnp.float32), block_sums, precision=lax.Precision.HIGHEST)
    seq_totals = sent_and_summed(seq_part, "dp", 0)
    own_lengths = lax.dynamic_slice_in_dim(lengths, device_rank * seq_local, seq_local).astype(
        jnp.float32
    )
    scores = seq_totals / own_lengths[:, None]
    worst_case = jnp.min(scores, axis=1)
    head_mean = jnp.mean(scores, axis=1)
    spread = jnp.mean((scores - head_mean[:, None]) ** 2, axis=1)
    total_seqs = float(seq_count)
    moment_sums = packed_total(
        (
            jnp.sum(spread),
            jnp.sum(worst_case),
            jnp.sum(worst_case * worst_case),
            jnp.sum(worst_case * spread),
            jnp.sum(spread * spread),
        ),
        "dp",
    )
    penalty_scale = moment_sums[0] / total_seqs + stat_epsilon
    conservative = worst_case - spread / penalty_scale
    first_sum = moment_sums[1] - moment_sums[0] / penalty_scale
    second = (
        moment_sums[2]
        - 2.0 * moment_sums[3] / penalty_scale
        + moment_sums[4] / (penalty_scale * penalty_scale)
    )
    centre = first_sum / total_seqs
    variance = second / total_seqs - centre * centre
    advantages = (conservative - centre) * lax.rsqrt(variance + stat_epsilon)
    return (token_rewards, advantages)


def solution(mesh):
    return jax.shard_map(
        local,
        mesh=mesh,
        in_specs=(
            P("dp", None, "mp"),
            P("dp", None, "mp"),
            P(None, "mp"),
            P("mp"),
            P("mp", None),
            P(),
            P(),
            P(),
        ),
        out_specs=(P("dp", None, None), P("dp")),
        check_vma=False,
    )
```

profile of v0, /device:TPU:1, one launch (start us, length us, event | category | flops | bytes accessed | tf_op | source)
XLA Modules:
  0.0 305.1 jit_solution(17338030331236136521)
XLA Ops:
  7.2 0.0 copy-start
  7.2 0.0 all-gather.2.cloned.1.call-start
  7.2 0.7 all-gather.2.cloned.1.call-update
  7.9 0.8 fusion.29
  8.7 0.2 convert_reduce_fusion.2
  8.9 101.2 %all-gather.2.cloned.1.call-done = bf16[15,128,2048]{2,1,0:T(8,128)(2,1)} async-done(((bf16[15,128,256]{2,1,0:T(8,128)(2,1)}), bf16[15,128,2048]{2,1,0:T(8,128)(2,1)}) %all-gather.2.cloned.1.call-update) | async-done | bytes 7864336 | tf_op jit(solution)/shard_map/all_gather | solution.py:84
  110.1 0.0 copy-done
  110.1 5.7 %add_convert_fusion = bf16[15,128,256]{2,1,0:T(8,128)(2,1)S(1)} fusion(bf16[15,128,256]{2,1,0:T(8,128)(2,1)} %param.8, bf16[15,128,2048]{2,1,0:T(8,128)(2,1)} %all-gather.2.cloned.1.call-done, bf16[2048,256]{1,0:T(8,128)(2,1)S(1)} %copy-done), kind=kOutput, calls=%fused_computation.3 | convolution fusion | flops 2014740480 | bytes 10878976 | tf_op jit(solution)/shard_map/btf,fc->btc/dot_general | solution.py:82
  115.8 1.4 convolution_convert_fusion
  117.1 4.4 %copy.29 = bf16[64,128,256]{2,1,0:T(8,128)(2,1)} copy(bf16[64,128,256]{2,0,1:T(8,128)(2,1)S(1)} %convolution_convert_fusion) | data formatting | bytes 8388608 | tf_op jit(solution)/shard_map/convert_element_type | solution.py:90
  121.5 0.0 copy-start.1
  121.5 0.0 copy-start.2
  121.5 0.0 copy-start.4
  121.5 0.0 copy-start.5
  121.5 13.3 %all-to-all-start = ((bf16[64,128,256]{2,1,0:T(8,128)(2,1)}), bf16[64,128,256]{2,1,0:T(8,128)(2,1)}, u32[]{:S(2)}, u32[]{:S(2)}) async-start(bf16[64,128,256]{2,1,0:T(8,128)(2,1)} %copy.29), calls=%async_computation | async-start | bytes 8388608 | tf_op jit(solution)/shard_map/all_to_all | solution.py:89
  134.8 0.0 copy-start.3
  134.9 0.0 copy-done.1
  134.9 0.0 copy-done.2
  134.9 0.2 fusion.3
  135.1 0.2 convert_reduce_fusion
  135.4 94.2 %all-to-all-done = bf16[64,128,256]{2,1,0:T(8,128)(2,1)} async-done(((bf16[64,128,256]{2,1,0:T(8,128)(2,1)}), bf16[64,128,256]{2,1,0:T(8,128)(2,1)}, u32[]{:S(2)}, u32[]{:S(2)}) %all-to-all-start) | async-done | bytes 4194336 | tf_op jit(solution)/shard_map/all_to_all | solution.py:89
  229.5 2.8 gather_fusion
  232.3 0.3 multiply_reduce_fusion
  232.7 0.0 copy-done.4
  232.7 0.0 copy-done.5
  232.7 0.7 convolution_bitcast_fusion
  233.4 0.9 broadcast_in_dim.89
  234.3 3.9 %all-to-all-start.1 = ((f32[8,1,11520]{2,1,0:T(1,128)}), f32[8,1,11520]{2,1,0:T(1,128)S(1)}, u32[]{:S(2)}, u32[]{:S(2)}) async-start(f32[8,1,11520]{2,1,0:T(1,128)} %broadcast_in_dim.89), calls=%async_computation.1 | async-start | bytes 737280 | tf_op jit(solution)/shard_map/all_to_all | solution.py:13
  238.2 0.0 copy-done.3
  238.2 0.2 select_reduce_fusion
  238.4 11.5 %all-to-all-done.1 = f32[8,1,11520]{2,1,0:T(1,128)S(1)} async-done(((f32[8,1,11520]{2,1,0:T(1,128)}), f32[8,1,11520]{2,1,0:T(1,128)S(1)}, u32[]{:S(2)}, u32[]{:S(2)}) %all-to-all-start.1) | async-done | bytes 368672 | tf_op jit(solution)/shard_map/all_to_all | solution.py:13
  249.9 0.3 reduce_sum.169
  250.2 0.1 fusion.15
  250.2 0.6 fusion.34
  250.9 0.2 fusion.7
  251.1 0.8 copy.32
  251.9 9.6 %all-to-all-start.2 = ((f32[64,6,8]{2,1,0:T(8,128)}), f32[64,6,8]{2,1,0:T(8,128)S(1)}, u32[]{:S(2)}, u32[]{:S(2)}) async-start(f32[64,6,8]{2,1,0:T(8,128)} %copy.32), calls=%async_computation.2 | async-start | bytes 524288 | tf_op jit(solution)/shard_map/all_to_all | solution.py:36
  261.6 0.1 dynamic-slice_convert_fusion
  261.6 13.0 %all-to-all-done.2 = f32[64,6,8]{2,1,0:T(8,128)S(1)} async-done(((f32[64,6,8]{2,1,0:T(8,128)}), f32[64,6,8]{2,1,0:T(8,128)S(1)}, u32[]{:S(2)}, u32[]{:S(2)}) %all-to-all-start.2) | async-done | bytes 12320 | tf_op jit(solution)/shard_map/all_to_all | solution.py:36
  274.6 0.1 reduce_sum.174
  274.7 0.2 fusion.32
  274.9 0.2 multiply_reduce_fusion.1
  275.1 0.7 multiply_reduce_fusion.2
  275.8 3.2 %concatenate.7 = f32[5]{0:T(128)S(1)} concatenate(f32[1]{0:T(128)} %bitcast.13, f32[1]{0:T(128)} %bitcast.14, f32[1]{0:T(128)} %bitcast.15, f32[1]{0:T(128)} %bitcast.16, f32[1]{0:T(128)} %bitcast.17), dimensions={0} | concatenate | bytes 40 | tf_op jit(solution)/shard_map/concatenate | solution.py:25
  279.1 14.0 %all_to_all.22 = f32[64,1,5]{2,1,0:T(1,128)S(1)} all-to-all(f32[64,1,5]{2,1,0:T(1,128)S(1)} %broadcast_in_dim.93), channel_id=1, replica_groups=mesh['dp'=64,'mp'=8] {'dp'}, dimensions={0} | all-to-all | bytes 2560 | tf_op jit(solution)/shard_map/all_to_all | solution.py:13
  293.1 0.1 reduce_sum.182
  293.1 0.7 fusion.36
  297.7 0.5 subtract_multiply_fusion
  (12 shorter events, 0.1 us)
Async XLA Ops:
  7.2 102.9 %copy-start = (bf16[2048,256]{1,0:T(8,128)(2,1)S(1)}, bf16[2048,256]{1,0:T(8,128)(2,1)}, u32[]{:S(2)}) copy-start(bf16[2048,256]{1,0:T(8,128)(2,1)} %param.10) | copy-start | bytes 3145732
  7.2 102.9 %all-gather.2.cloned.1.call-start = ((), (), s32[]{:S(2)}) async-start(), calls=%async_computation.4 | async-start | bytes 8847360 | tf_op jit(solution)/shard_map/all_gather | solution.py:84
  121.5 13.3 %copy-start.1 = (s32[960]{0:T(1024)S(1)}, s32[960]{0:T(1024)}, u32[]{:S(2)}) copy-start(s32[960]{0:T(1024)} %param.14) | copy-start | bytes 11524
  121.5 13.3 %copy-start.2 = (s32[960]{0:T(1024)S(1)}, s32[960]{0:T(1024)}, u32[]{:S(2)}) copy-start(s32[960]{0:T(1024)} %param.13) | copy-start | bytes 11524
  121.5 111.1 %copy-start.4 = (f32[256,8]{0,1:T(8,128)S(1)}, f32[256,8]{0,1:T(8,128)}, u32[]{:S(2)}) copy-start(f32[256,8]{0,1:T(8,128)} %param.12) | copy-start | bytes 24580
  121.5 111.1 %copy-start.5 = (f32[256]{0:T(256)S(1)}, f32[256]{0:T(256)}, u32[]{:S(2)}) copy-start(f32[256]{0:T(256)} %param.11) | copy-start | bytes 3076
  121.5 108.0 %all-to-all-start = ((bf16[64,128,256]{2,1,0:T(8,128)(2,1)}), bf16[64,128,256]{2,1,0:T(8,128)(2,1)}, u32[]{:S(2)}, u32[]{:S(2)}) async-start(bf16[64,128,256]{2,1,0:T(8,128)(2,1)} %copy.29), calls=%async_computation | async-start | bytes 8388608 | tf_op jit(solution)/shard_map/all_to_all | solution.py:89
  134.8 103.4 %copy-start.3 = (s32[384]{0:T(512)S(1)}, s32[384]{0:T(512)}, u32[]{:S(2)}) copy-start(s32[384]{0:T(512)} %param.15) | copy-start | bytes 4612
  234.3 15.6 %all-to-all-start.1 = ((f32[8,1,11520]{2,1,0:T(1,128)}), f32[8,1,11520]{2,1,0:T(1,128)S(1)}, u32[]{:S(2)}, u32[]{:S(2)}) async-start(f32[8,1,11520]{2,1,0:T(1,128)} %broadcast_in_dim.89), calls=%async_computation.1 | async-start | bytes 737280 | tf_op jit(solution)/shard_map/all_to_all | solution.py:13
  251.9 22.7 %all-to-all-start.2 = ((f32[64,6,8]{2,1,0:T(8,128)}), f32[64,6,8]{2,1,0:T(8,128)S(1)}, u32[]{:S(2)}, u32[]{:S(2)}) async-start(f32[64,6,8]{2,1,0:T(8,128)} %copy.32), calls=%async_computation.2 | async-start | bytes 524288 | tf_op jit(solution)/shard_map/all_to_all | solution.py:36
Sparse Core Ops, SparseCore 0:
  10.0 100.0 all-gather.1
where the time goes:
time: 306 us; the launch traced here: 305 us
  waiting for transfers between devices  221 us (72%)
  starting transfers between devices  26.8 us (9%)
  between operations  18.1 us (6%)
  blocking collectives  14 us (5%)
  local copies, waits for them, and re-layouts  12.9 us (4%)
  matrix products  7.93 us (3%)
  other arithmetic  4.83 us (2%)
    all_gather x1, waiting for transfers between devices, local(): lax.all_gather(attn_out, 'mp', axis=2, tiled=True)  101 us
    all_to_all x1, waiting for transfers between devices, local(): lax.all_to_all(jnp.einsum('rj,jtf->rtf', selector, local_resid, preferred...  94.2 us
    all_to_all x1, blocking collectives, sent_to_all(): return lax.all_to_all(copies, axis, split_axis=0, concat_axis=0, tiled=True)  14 us
    all_to_all x1, starting transfers between devices, local(): lax.all_to_all(jnp.einsum('rj,jtf->rtf', selector, local_resid, preferred...  13.3 us
    all_to_all x1, waiting for transfers between devices, sent_and_summed(): lax.all_to_all(parts, axis, split_axis=0, concat_axis=0, tiled=True)  13 us
    all_to_all x1, waiting for transfers between devices, sent_to_all(): return lax.all_to_all(copies, axis, split_axis=0, concat_axis=0, tiled=True)  11.5 us
    all_to_all x1, starting transfers between devices, sent_and_summed(): lax.all_to_all(parts, axis, split_axis=0, concat_axis=0, tiled=True)  9.64 us
  transfers between devices with their start and end apart: 4, of which 4 were waited for; matrix products, arithmetic and copies ran while one was open for 1% of the time, Pallas kernels for 0%

commit v1 on v0

--- a/solution.py
+++ b/solution.py
@@ -6,6 +6,29 @@
 OWN_CAP = 10
 norm_epsilon = 1e-05
 stat_epsilon = 1e-06
+
+
+def joined_along(pieces, dim):
+    pieces = jnp.moveaxis(pieces, 0, dim)
+    lengths = pieces.shape
+    return pieces.reshape(*lengths[:dim], lengths[dim] * lengths[dim + 1], *lengths[dim + 2 :])
+
+
+def grow_blocks(shard, axis):
+    size, here = (lax.axis_size(axis), lax.axis_index(axis))
+    blocks, bit = (shard[None], 1)
+    while bit < size:
+        partner_block = lax.ppermute(blocks, axis, [(i, i ^ bit) for i in range(size)])
+        low = here & bit == 0
+        blocks = jnp.concatenate(
+            [jnp.where(low, blocks, partner_block), jnp.where(low, partner_block, blocks)]
+        )
+        bit *= 2
+    return blocks
+
+
+def collect(x, axis, dim):
+    return joined_along(grow_blocks(x, axis), dim)
 
 
 def sent_to_all(value, axis):
@@ -80,10 +103,7 @@
     own_length = jnp.sum(jnp.where(member, lengths[:, None], 0), axis=0)
     valid_tokens = jnp.minimum(block_len, own_length - block_len * seq_rank)
     projected = jnp.einsum(
-        "btf,fc->btc",
-        lax.all_gather(attn_out, "mp", axis=2, tiled=True),
-        out_proj,
-        preferred_element_type=jnp.float32,
+        "btf,fc->btc", collect(attn_out, "mp", 2), out_proj, preferred_element_type=jnp.float32
     )
     local_resid = (hidden.astype(jnp.float32) + projected).astype(jnp.bfloat16)
     moved_resid = lax.all_to_all(

time: 306 us -> 504 us (1.65)
  waiting for transfers between devices: 221 us -> 390 us
  starting transfers between devices: 26.8 us -> 50 us
  other arithmetic: 4.83 us -> 21.5 us
  between operations: 18.1 us -> 4.79 us
    ppermute x0 -> x3, waiting for transfers between devices: none -> 271 us  [grow_blocks(): lax.ppermute(blocks, axis, [(i, i ^ bit) for i in range(size)])]
    all_gather x1 -> x0, waiting for transfers between devices: 101 us -> none  [local(): lax.all_gather(attn_out, 'mp', axis=2, tiled=True)]
    ppermute x0 -> x3, starting transfers between devices: none -> 22.8 us  [grow_blocks(): lax.ppermute(blocks, axis, [(i, i ^ bit) for i in range(size)])]
    concatenate x0 -> x3, other arithmetic: none -> 9.78 us  [grow_blocks(): jnp.concatenate([jnp.where(low, blocks, partner_block), jnp.where(low, pa...]
    select_n x0 -> x3, other arithmetic: none -> 7.59 us  [grow_blocks(): jnp.where(low, blocks, partner_block)]
  transfers between devices with their start and end apart: 4 -> 6, of which waited for: 4 -> 6; matrix products, arithmetic and copies ran while one was open for 1% -> 0% of each run, Pallas kernels for 0% -> 0%
where the time goes in v1:
time: 504 us; the launch traced here: 503 us
  waiting for transfers between devices  390 us (77%)
  starting transfers between devices  50 us (10%)
  other arithmetic  21.5 us (4%)
  local copies, waits for them, and re-layouts  15.6 us (3%)
  blocking collectives  14 us (3%)
  matrix products  7.76 us (2%)
    ppermute x3, waiting for transfers between devices, grow_blocks(): lax.ppermute(blocks, axis, [(i, i ^ bit) for i in range(size)])  271 us
    all_to_all x1, waiting for transfers between devices, local(): lax.all_to_all(jnp.einsum('rj,jtf->rtf', selector, local_resid, preferred...  94.2 us
    ppermute x3, starting transfers between devices, grow_blocks(): lax.ppermute(blocks, axis, [(i, i ^ bit) for i in range(size)])  22.8 us
    all_to_all x1, blocking collectives, sent_to_all(): return lax.all_to_all(copies, axis, split_axis=0, concat_axis=0, tiled=True)  14 us
    all_to_all x1, waiting for transfers between devices, sent_and_summed(): lax.all_to_all(parts, axis, split_axis=0, concat_axis=0, tiled=True)  13 us
    all_to_all x1, starting transfers between devices, local(): lax.all_to_all(jnp.einsum('rj,jtf->rtf', selector, local_resid, preferred...  12.5 us
    all_to_all x1, waiting for transfers between devices, sent_to_all(): return lax.all_to_all(copies, axis, split_axis=0, concat_axis=0, tiled=True)  11.5 us
  transfers between devices with their start and end apart: 6, of which 6 were waited for; matrix products, arithmetic and copies ran while one was open for 0% of the time, Pallas kernels for 0%

profile of v1, /device:TPU:1, one launch (start us, length us, event | category | flops | bytes accessed | tf_op | source)
XLA Modules:
  0.0 503.3 jit_solution(7355960474131697853)
XLA Ops:
  0.6 1.7 copy.35
  2.3 4.8 collective-permute-start
  7.2 17.4 %collective-permute-done = bf16[1,15,128,256]{2,3,0,1:T(8,128)(2,1)S(1)} collective-permute-done((bf16[1,15,128,256]{2,3,0,1:T(8,128)(2,1)S(1)}, bf16[1,15,128,256]{2,3,0,1:T(8,128)(2,1)S(1)}, u32[]{:S(2)}, u32[]{:S(2)}) %collective-permute-start) | collective-permute-done | bytes 983072 | tf_op jit(solution)/shard_map/ppermute | solution.py:21
  24.6 0.1 broadcast_select_fusion.5
  24.7 0.9 copy-done.2
  25.7 0.2 pad_maximum_fusion.2
  25.9 0.1 copy-done.3
  26.0 9.8 %collective-permute-start.1 = (bf16[2,15,128,256]{2,3,0,1:T(8,128)(2,1)S(1)}, bf16[2,15,128,256]{2,3,0,1:T(8,128)(2,1)}, u32[]{:S(2)}, u32[]{:S(2)}) collective-permute-start(bf16[2,15,128,256]{2,3,0,1:T(8,128)(2,1)S(1)} %pad_maximum_fusion.2), channel_id=1, source_target_pairs={{0,2},{1,3},{2,0},{3,1},{4,6},{5,7},{6,4},{7,5},{8,10},{9,11},{10,... | collective-permute-start | bytes 5898248 | tf_op jit(solution)/shard_map/ppermute | solution.py:21
  35.8 84.6 %collective-permute-done.1 = bf16[2,15,128,256]{2,3,0,1:T(8,128)(2,1)} collective-permute-done((bf16[2,15,128,256]{2,3,0,1:T(8,128)(2,1)S(1)}, bf16[2,15,128,256]{2,3,0,1:T(8,128)(2,1)}, u32[]{:S(2)}, u32[]{:S(2)}) %collective-permute-start.1) | collective-permute-done | bytes 1966112 | tf_op jit(solution)/shard_map/ppermute | solution.py:21
  120.4 2.3 broadcast_select_fusion.3
  122.8 2.5 pad_maximum_fusion.1
  125.3 8.1 %collective-permute-start.2 = (bf16[4,15,128,256]{2,3,0,1:T(8,128)(2,1)}, bf16[4,15,128,256]{2,3,0,1:T(8,128)(2,1)}, u32[]{:S(2)}, u32[]{:S(2)}) collective-permute-start(bf16[4,15,128,256]{2,3,0,1:T(8,128)(2,1)} %pad_maximum_fusion.1), channel_id=1, source_target_pairs={{0,4},{1,5},{2,6},{3,7},{4,0},{5,1},{6,2},{7,3},{8,12},{9,13},{10,... | collective-permute-start | bytes 11796488 | tf_op jit(solution)/shard_map/ppermute | solution.py:21
  133.4 0.1 fusion.29
  133.5 0.2 convert_reduce_fusion.2
  133.7 168.9 %collective-permute-done.2 = bf16[4,15,128,256]{2,3,0,1:T(8,128)(2,1)} collective-permute-done((bf16[4,15,128,256]{2,3,0,1:T(8,128)(2,1)}, bf16[4,15,128,256]{2,3,0,1:T(8,128)(2,1)}, u32[]{:S(2)}, u32[]{:S(2)}) %collective-permute-start.2) | collective-permute-done | bytes 3932192 | tf_op jit(solution)/shard_map/ppermute | solution.py:21
  302.7 5.1 %broadcast_select_fusion.1 = (bf16[4,15,128,256]{2,3,0,1:T(8,128)(2,1)}, bf16[4,15,128,256]{2,3,0,1:T(8,128)(2,1)}) fusion(bf16[4,15,128,256]{2,3,0,1:T(8,128)(2,1)} %collective-permute-done.2, pred[]{:T(512)S(6)} %eq.103, bf16[2,15,128,256]{2,3,0,1:T(8,128)(2,1)} %copy-done.1, bf16[2,15,128,256]{2,3,0,1:T(8,128)(2,1)S(1)} %get-tuple-element.21), kind=kLoop, calls=%fused_computation.4 | loop fusion | flops 5898240 | bytes 15728641 | tf_op jit(solution)/shard_map/jit(_where)/select_n | solution.py:24
  307.8 7.1 %pad_maximum_fusion = bf16[8,15,128,256]{2,3,0,1:T(8,128)(2,1)} fusion(bf16[4,15,128,256]{2,3,0,1:T(8,128)(2,1)} %get-tuple-element.20, bf16[4,15,128,256]{2,3,0,1:T(8,128)(2,1)} %get-tuple-element.19), kind=kLoop, calls=%fused_computation.1 | loop fusion | flops 3932160 | bytes 15728640 | tf_op jit(solution)/shard_map/concatenate | solution.py:23
  314.9 5.5 %add_convert_fusion = bf16[15,128,256]{2,1,0:T(8,128)(2,1)S(1)} fusion(bf16[15,128,256]{2,1,0:T(8,128)(2,1)S(1)} %copy-done.4, bf16[15,128,2048]{1,2,0:T(8,128)(2,1)} %bitcast.59, bf16[2048,256]{1,0:T(8,128)(2,1)S(1)} %copy-done), kind=kOutput, calls=%fused_computation.8 | convolution fusion | flops 2014740480 | bytes 10878976 | tf_op jit(solution)/shard_map/btf,fc->btc/dot_general | solution.py:105
  320.4 1.4 convolution_convert_fusion
  321.8 4.4 copy.38
  326.2 12.5 %all-to-all-start = ((bf16[64,128,256]{2,1,0:T(8,128)(2,1)}), bf16[64,128,256]{2,1,0:T(8,128)(2,1)}, u32[]{:S(2)}, u32[]{:S(2)}) async-start(bf16[64,128,256]{2,1,0:T(8,128)(2,1)} %copy.38), calls=%async_computation | async-start | bytes 8388608 | tf_op jit(solution)/shard_map/all_to_all | solution.py:109
  338.7 0.2 fusion.3
  338.9 0.2 convert_reduce_fusion
  339.2 94.2 %all-to-all-done = bf16[64,128,256]{2,1,0:T(8,128)(2,1)} async-done(((bf16[64,128,256]{2,1,0:T(8,128)(2,1)}), bf16[64,128,256]{2,1,0:T(8,128)(2,1)}, u32[]{:S(2)}, u32[]{:S(2)}) %all-to-all-start) | async-done | bytes 4194336 | tf_op jit(solution)/shard_map/all_to_all | solution.py:109
  433.4 2.8 gather_fusion
  436.1 0.3 multiply_reduce_fusion
  436.5 0.7 convolution_bitcast_fusion
  437.2 0.9 broadcast_in_dim.93
  438.1 5.2 %all-to-all-start.1 = ((f32[8,1,11520]{2,1,0:T(1,128)}), f32[8,1,11520]{2,1,0:T(1,128)S(1)}, u32[]{:S(2)}, u32[]{:S(2)}) async-start(f32[8,1,11520]{2,1,0:T(1,128)} %broadcast_in_dim.93), calls=%async_computation.1 | async-start | bytes 737280 | tf_op jit(solution)/shard_map/all_to_all | solution.py:36
  443.3 0.2 select_reduce_fusion
  443.5 11.5 %all-to-all-done.1 = f32[8,1,11520]{2,1,0:T(1,128)S(1)} async-done(((f32[8,1,11520]{2,1,0:T(1,128)}), f32[8,1,11520]{2,1,0:T(1,128)S(1)}, u32[]{:S(2)}, u32[]{:S(2)}) %all-to-all-start.1) | async-done | bytes 368672 | tf_op jit(solution)/shard_map/all_to_all | solution.py:36
  455.0 0.3 reduce_sum.169
  455.3 0.1 fusion.15
  455.3 0.6 fusion.34
  456.0 0.2 fusion.7
  456.2 0.8 copy.41
  457.0 9.6 %all-to-all-start.2 = ((f32[64,6,8]{2,1,0:T(8,128)}), f32[64,6,8]{2,1,0:T(8,128)S(1)}, u32[]{:S(2)}, u32[]{:S(2)}) async-start(f32[64,6,8]{2,1,0:T(8,128)} %copy.41), calls=%async_computation.2 | async-start | bytes 524288 | tf_op jit(solution)/shard_map/all_to_all | solution.py:59
  466.7 0.1 dynamic-slice_convert_fusion
  466.7 13.0 %all-to-all-done.2 = f32[64,6,8]{2,1,0:T(8,128)S(1)} async-done(((f32[64,6,8]{2,1,0:T(8,128)}), f32[64,6,8]{2,1,0:T(8,128)S(1)}, u32[]{:S(2)}, u32[]{:S(2)}) %all-to-all-start.2) | async-done | bytes 12320 | tf_op jit(solution)/shard_map/all_to_all | solution.py:59
  479.7 0.1 reduce_sum.174
  479.8 0.2 fusion.32
  480.0 0.2 multiply_reduce_fusion.1
  480.2 0.7 multiply_reduce_fusion.2
  480.9 3.2 concatenate.19
  484.2 14.0 %all_to_all.22 = f32[64,1,5]{2,1,0:T(1,128)S(1)} all-to-all(f32[64,1,5]{2,1,0:T(1,128)S(1)} %broadcast_in_dim.97), channel_id=1, replica_groups=mesh['dp'=64,'mp'=8] {'dp'}, dimensions={0} | all-to-all | bytes 2560 | tf_op jit(solution)/shard_map/all_to_all | solution.py:36
  498.2 0.1 reduce_sum.182
  498.2 0.7 fusion.36
  502.8 0.5 subtract_multiply_fusion
  (30 shorter events, 0.2 us)
Async XLA Ops:
  0.6 314.3 %copy-start = (bf16[2048,256]{1,0:T(8,128)(2,1)S(1)}, bf16[2048,256]{1,0:T(8,128)(2,1)}, u32[]{:S(2)}) copy-start(bf16[2048,256]{1,0:T(8,128)(2,1)} %param.10) | copy-start | bytes 3145732
  2.3 22.3 %collective-permute-start = (bf16[1,15,128,256]{2,3,0,1:T(8,128)(2,1)S(1)}, bf16[1,15,128,256]{2,3,0,1:T(8,128)(2,1)S(1)}, u32[]{:S(2)}, u32[]{:S(2)}) collective-permute-start(bf16[1,15,128,256]{2,3,0,1:T(8,128)(2,1)S(1)} %bitcast.60), channel_id=1, source_target_pairs={{0,1},{1,0},{2,3},{3,2},{4,5},{5,4},{6,7},{7,6},{8,9},{9,8},{10,11... | collective-permute-start | bytes 2949128 | tf_op jit(solution)/shard_map/ppermute | solution.py:21
  24.7 0.9 copy-start.2
  24.7 1.3 copy-start.3
  26.0 94.4 %collective-permute-start.1 = (bf16[2,15,128,256]{2,3,0,1:T(8,128)(2,1)S(1)}, bf16[2,15,128,256]{2,3,0,1:T(8,128)(2,1)}, u32[]{:S(2)}, u32[]{:S(2)}) collective-permute-start(bf16[2,15,128,256]{2,3,0,1:T(8,128)(2,1)S(1)} %pad_maximum_fusion.2), channel_id=1, source_target_pairs={{0,2},{1,3},{2,0},{3,1},{4,6},{5,7},{6,4},{7,5},{8,10},{9,11},{10,... | collective-permute-start | bytes 5898248 | tf_op jit(solution)/shard_map/ppermute | solution.py:21
  122.8 2.5 copy-start.1
  122.8 10.6 %copy-start.5 = (s32[960]{0:T(1024)S(1)}, s32[960]{0:T(1024)}, u32[]{:S(2)}) copy-start(s32[960]{0:T(1024)} %param.14) | copy-start | bytes 11524
  125.3 177.4 %collective-permute-start.2 = (bf16[4,15,128,256]{2,3,0,1:T(8,128)(2,1)}, bf16[4,15,128,256]{2,3,0,1:T(8,128)(2,1)}, u32[]{:S(2)}, u32[]{:S(2)}) collective-permute-start(bf16[4,15,128,256]{2,3,0,1:T(8,128)(2,1)} %pad_maximum_fusion.1), channel_id=1, source_target_pairs={{0,4},{1,5},{2,6},{3,7},{4,0},{5,1},{6,2},{7,3},{8,12},{9,13},{10,... | collective-permute-start | bytes 11796488 | tf_op jit(solution)/shard_map/ppermute | solution.py:21
  307.8 7.1 %copy-start.4 = (bf16[15,128,256]{2,1,0:T(8,128)(2,1)S(1)}, bf16[15,128,256]{2,1,0:T(8,128)(2,1)}, u32[]{:S(2)}) copy-start(bf16[15,128,256]{2,1,0:T(8,128)(2,1)} %param.8) | copy-start | bytes 2949124
  326.2 12.5 %copy-start.6 = (s32[960]{0:T(1024)S(1)}, s32[960]{0:T(1024)}, u32[]{:S(2)}) copy-start(s32[960]{0:T(1024)} %param.13) | copy-start | bytes 11524
  326.2 110.3 %copy-start.8 = (f32[256,8]{0,1:T(8,128)S(1)}, f32[256,8]{0,1:T(8,128)}, u32[]{:S(2)}) copy-start(f32[256,8]{0,1:T(8,128)} %param.12) | copy-start | bytes 24580
  326.2 110.3 %copy-start.9 = (f32[256]{0:T(256)S(1)}, f32[256]{0:T(256)}, u32[]{:S(2)}) copy-start(f32[256]{0:T(256)} %param.11) | copy-start | bytes 3076
  326.2 107.2 %all-to-all-start = ((bf16[64,128,256]{2,1,0:T(8,128)(2,1)}), bf16[64,128,256]{2,1,0:T(8,128)(2,1)}, u32[]{:S(2)}, u32[]{:S(2)}) async-start(bf16[64,128,256]{2,1,0:T(8,128)(2,1)} %copy.38), calls=%async_computation | async-start | bytes 8388608 | tf_op jit(solution)/shard_map/all_to_all | solution.py:109
  338.6 104.7 %copy-start.7 = (s32[384]{0:T(512)S(1)}, s32[384]{0:T(512)}, u32[]{:S(2)}) copy-start(s32[384]{0:T(512)} %param.15) | copy-start | bytes 4612
  438.1 16.8 %all-to-all-start.1 = ((f32[8,1,11520]{2,1,0:T(1,128)}), f32[8,1,11520]{2,1,0:T(1,128)S(1)}, u32[]{:S(2)}, u32[]{:S(2)}) async-start(f32[8,1,11520]{2,1,0:T(1,128)} %broadcast_in_dim.93), calls=%async_computation.1 | async-start | bytes 737280 | tf_op jit(solution)/shard_map/all_to_all | solution.py:36
  457.0 22.7 %all-to-all-start.2 = ((f32[64,6,8]{2,1,0:T(8,128)}), f32[64,6,8]{2,1,0:T(8,128)S(1)}, u32[]{:S(2)}, u32[]{:S(2)}) async-start(f32[64,6,8]{2,1,0:T(8,128)} %copy.41), calls=%async_computation.2 | async-start | bytes 524288 | tf_op jit(solution)/shard_map/all_to_all | solution.py:59
